TPU v7x, 32 devices: a whole 2x2x4 slice. The times are simulated.
32 devices in a mesh: fsdp: 2 (over y), trow: 4 (over x, core), tcol: 4 (over z).
Axes of the slice: x: 2, y: 2, z: 4, core: 2. Of those that a mesh axis runs over, the one named last changes fastest.
Arguments:
- tokens: bfloat16 [512, 4096], P('fsdp', 'tcol'), may hold values from -100 to 100
- w_up: bfloat16 [4096, 16384], P('tcol', ('fsdp', 'trow')), may hold values from -0.1875 to 0.1875
- w_down: bfloat16 [16384, 4096], P(('fsdp', 'trow'), 'tcol'), may hold values from -0.046875 to 0.046875
- cotangent: bfloat16 [512, 4096], P('fsdp', 'tcol'), may hold values from -6 to 6
Outputs:
- mixed: bfloat16 [512, 4096], P('fsdp', 'tcol')
- input_gradient: bfloat16 [512, 4096], P('fsdp', 'tcol')
- grad_up: bfloat16 [4096, 16384], P('tcol', ('fsdp', 'trow'))
- grad_down: bfloat16 [16384, 4096], P(('fsdp', 'trow'), 'tcol')
All inputs are finite; a program needn't handle non-finite values.
Results may differ from a plain program's by a relative error of at most 0.02.
Values may be sent and summed in bfloat16 or wider, within the bound.
A program may use at most 128 MiB of HBM per device.

v0:
```python
import jax
import jax.numpy as jnp
from jax import lax
from jax.sharding import PartitionSpec as P


def gelu_value(pre):
    phi = 0.5 * (1.0 + jax.scipy.special.erf(pre * 0.7071067811865476))
    return pre * phi


def gelu_slope(pre):
    phi = 0.5 * (1.0 + jax.scipy.special.erf(pre * 0.7071067811865476))
    return phi + pre * jnp.exp(-0.5 * pre * pre) * 0.3989422804014327


def contract(left, right, left_dim, right_dim):
    return lax.dot_general(
        left, right, (((left_dim,), (right_dim,)), ((), ())), preferred_element_type=jnp.float32
    )


def local(tokens, w_up, w_down, cotangent):
    width = tokens.shape[1] * lax.axis_size("tcol")
    input_float = tokens.astype(jnp.float32)
    sum_one, sum_two = lax.psum(
        (jnp.sum(input_float, axis=1), jnp.sum(input_float * input_float, axis=1)), "tcol"
    )
    token_mean = sum_one / width
    var = sum_two / width - token_mean * token_mean
    inverse_stddev = lax.rsqrt(var + 1e-05)
    centered_scaled = (input_float - token_mean[:, None]) * inverse_stddev[:, None]
    normalized_rows = centered_scaled.astype(jnp.bfloat16)
    up_full, down_full = (
        lax.all_gather(w_up, "fsdp", axis=1, tiled=True),
        lax.all_gather(w_down, "fsdp", axis=0, tiled=True),
    )
    pre_full = lax.psum(
        jnp.dot(normalized_rows, up_full, preferred_element_type=jnp.float32).astype(jnp.bfloat16),
        "tcol",
    ).astype(jnp.float32)
    hidden = gelu_value(pre_full).astype(jnp.bfloat16)
    branch = lax.psum(
        jnp.dot(hidden, down_full, preferred_element_type=jnp.float32).astype(jnp.bfloat16), "trow"
    ).astype(jnp.float32)
    mixed = (input_float + branch).astype(jnp.bfloat16)
    down_part = contract(hidden, cotangent, 0, 0)
    grad_down = lax.psum_scatter(
        down_part.astype(jnp.bfloat16), "fsdp", scatter_dimension=0, tiled=True
    )
    dhid = lax.psum(contract(cotangent, down_full, 1, 1).astype(jnp.bfloat16), "tcol").astype(
        jnp.float32
    )
    dpre = (dhid * gelu_slope(pre_full)).astype(jnp.bfloat16)
    up_part = contract(normalized_rows, dpre, 0, 0)
    grad_up = lax.psum_scatter(
        up_part.astype(jnp.bfloat16), "fsdp", scatter_dimension=1, tiled=True
    )
    normed_gradient = lax.psum(contract(dpre, up_full, 1, 1).astype(jnp.bfloat16), "trow").astype(
        jnp.float32
    )
    mean_first, mean_second = lax.psum(
        (jnp.sum(normed_gradient, axis=1), jnp.sum(normed_gradient * centered_scaled, axis=1)),
        "tcol",
    )
    first_moment = mean_first / width
    second_moment = mean_second / width
    input_gradient = cotangent.astype(jnp.float32) + inverse_stddev[:, None] * (
        normed_gradient - first_moment[:, None] - centered_scaled * second_moment[:, None]
    )
    return (mixed, input_gradient.astype(jnp.bfloat16), grad_up, grad_down)


def solution(mesh):
    return jax.shard_map(
        local,
        mesh=mesh,
        in_specs=(
            P("fsdp", "tcol"),
            P("tcol", ("fsdp", "trow")),
            P(("fsdp", "trow"), "tcol"),
            P("fsdp", "tcol"),
        ),
        out_specs=(
            P("fsdp", "tcol"),
            P("fsdp", "tcol"),
            P("tcol", ("fsdp", "trow")),
            P(("fsdp", "trow"), "tcol"),
        ),
        check_vma=False,
    )
```

profile of v0, /device:TPU:0, one launch (start us, length us, event | category | flops | bytes accessed | tf_op | source)
XLA Modules:
  0.0 644.7 jit_solution(2938886579183394449)
XLA Ops:
  7.2 0.0 all-gather.5.cloned.1.call-start
  7.2 0.7 all-gather.5.cloned.1.call-update
  7.9 0.0 all-gather.3.cloned.1.call-start
  8.0 0.7 all-gather.3.cloned.1.call-update
  8.7 0.0 all-reduce.7.cloned.1.call-start
  8.7 0.2 convert_reduce_fusion
  9.0 13.5 %all-reduce.1 = (f32[256]{0:T(256)S(1)}, f32[256]{0:T(256)S(1)}) all-reduce(f32[256]{0:T(256)S(1)} %get-tuple-element.7, f32[256]{0:T(256)S(1)} %get-tuple-element.6), channel_id=1, replica_groups=mesh['fsdp'=2,'trow'=4,'tcol'=4] {'tcol'}, use_global_device_ids=true, to_apply=%region_3.0 | all-reduce | flops 512 | bytes 4096 | tf_op jit(solution)/shard_map/psum | solution.py:26
  22.5 93.8 %all-gather.5.cloned.1.call-done = bf16[4096,1024]{1,0:T(8,128)(2,1)} async-done(((bf16[2048,1024]{1,0:T(8,128)(2,1)}), bf16[4096,1024]{1,0:T(8,128)(2,1)}) %all-gather.5.cloned.1.call-update) | async-done | bytes 8388624 | tf_op jit(solution)/shard_map/all_gather | solution.py:36
  116.3 7.1 %convolution_convert_fusion.2 = bf16[256,4096]{1,0:T(8,128)(2,1)} fusion(bf16[256,1024]{1,0:T(8,128)(2,1)S(1)} %copy-done.3, bf16[4096,1024]{1,0:T(8,128)(2,1)} %all-gather.5.cloned.1.call-done), kind=kOutput, calls=%fused_computation.7 | convolution fusion | flops 2148532224 | bytes 11010048 | tf_op jit(solution)/shard_map/dot_general | solution.py:18
  123.3 98.5 %all-gather.3.cloned.1.call-done = bf16[1024,4096]{1,0:T(8,128)(2,1)} async-done(((bf16[1024,2048]{1,0:T(8,128)(2,1)}), bf16[1024,4096]{1,0:T(8,128)(2,1)}) %all-gather.3.cloned.1.call-update) | async-done | bytes 8388624 | tf_op jit(solution)/shard_map/all_gather | solution.py:35
  221.8 7.1 %convolution_convert_fusion.3 = bf16[256,4096]{1,0:T(8,128)(2,1)} fusion(bf16[1024,4096]{1,0:T(8,128)(2,1)} %all-gather.3.cloned.1.call-done, bf16[256,1024]{1,0:T(8,128)(2,1)S(1)} %copy-done, f32[256]{0:T(256)S(1)} %get-tuple-element.19, f32[256]{0:T(256)S(1)} %get-tuple-element.18), kind=kOutput, calls=%fused_computation.8 | convolution fusion | flops 2149580800 | bytes 11012096 | tf_op jit(solution)/shard_map/dot_general | solution.py:39
  229.0 0.0 all-reduce.7.cloned.1.call-update
  229.0 0.0 all-reduce.9.cloned.1.call-start
  229.0 155.1 %all-reduce.7.cloned.1.call-done = (bf16[256,4096]{1,0:T(8,128)(2,1)}, bf16[256,4096]{1,0:T(8,128)(2,1)}) async-done(((bf16[256,4096]{1,0:T(8,128)(2,1)}, bf16[256,4096]{1,0:T(8,128)(2,1)}), (bf16[256,4096]{1,0:T(8,128)(2,1)}, bf16[256,4096]{1,0:T(8,128)(2,1)})) %all-reduce.7.cloned.1.call-update) | async-done | bytes 4194320 | tf_op jit(solution)/shard_map/psum | solution.py:38
  384.2 3.7 fusion.8
  387.9 0.0 slice-start.1
  387.9 6.8 %convolution_convert_fusion.5 = bf16[256,1024]{1,0:T(8,128)(2,1)} fusion(bf16[4096,1024]{1,0:T(8,128)(2,1)} %all-gather.5.cloned.1.call-done, bf16[256,4096]{1,0:T(8,128)(2,1)S(1)} %copy-done.1), kind=kOutput, calls=%fused_computation.26 | convolution fusion | flops 2154037248 | bytes 11010048 | tf_op jit(solution)/shard_map/dot_general | solution.py:44
  394.6 3.2 convolution_convert_fusion.4
  397.8 0.0 all-reduce.9.cloned.1.call-update
  397.8 0.2 reduce-scatter.3.cloned.1.call-start
  398.1 5.7 convolution_convert_fusion.1
  403.8 0.0 reduce-scatter.3.cloned.1.call-update
  403.8 0.0 reduce-scatter.5.cloned.1.call-start
  403.9 1.5 copy-done.2
  405.4 4.7 convolution_convert_fusion
  410.1 0.0 reduce-scatter.5.cloned.1.call-update
  410.1 23.2 %all-reduce.9.cloned.1.call-done = (bf16[256,1024]{1,0:T(8,128)(2,1)}, bf16[256,1024]{1,0:T(8,128)(2,1)}) async-done(((bf16[256,1024]{1,0:T(8,128)(2,1)}, bf16[256,1024]{1,0:T(8,128)(2,1)}), (bf16[256,1024]{1,0:T(8,128)(2,1)}, bf16[256,1024]{1,0:T(8,128)(2,1)})) %all-reduce.9.cloned.1.call-update) | async-done | bytes 1048592 | tf_op jit(solution)/shard_map/psum | solution.py:43
  433.3 1.5 convert_reduce_fusion.1
  434.7 11.7 %all-reduce = (f32[256]{0:T(256)S(1)}, f32[256]{0:T(256)S(1)}) all-reduce(f32[256]{0:T(256)S(1)} %get-tuple-element.5, f32[256]{0:T(256)S(1)} %get-tuple-element.4), channel_id=1, replica_groups=mesh['fsdp'=2,'trow'=4,'tcol'=4] {'tcol'}, use_global_device_ids=true, to_apply=%region_11.0 | all-reduce | flops 512 | bytes 4096 | tf_op jit(solution)/shard_map/psum | solution.py:62
  446.4 2.6 fusion.12
  449.0 86.8 %reduce-scatter.3.cloned.1.call-done = bf16[1024,2048]{1,0:T(8,128)(2,1)} async-done(((bf16[1024,4096]{1,0:T(8,128)(2,1)}), bf16[1024,2048]{1,0:T(8,128)(2,1)}) %reduce-scatter.3.cloned.1.call-update) | async-done | bytes 4194320 | tf_op jit(solution)/shard_map/reduce_scatter | solution.py:56
  535.8 102.1 %reduce-scatter.5.cloned.1.call-done = bf16[2048,1024]{1,0:T(8,128)(2,1)} async-done(((bf16[4096,1024]{1,0:T(8,128)(2,1)}), bf16[2048,1024]{1,0:T(8,128)(2,1)}) %reduce-scatter.5.cloned.1.call-update) | async-done | bytes 4194320 | tf_op jit(solution)/shard_map/reduce_scatter | solution.py:48
  (13 shorter events, 0.0 us)
Async XLA Ops:
  7.2 1.6 copy-start
  7.2 109.1 %copy-start.3 = (bf16[256,1024]{1,0:T(8,128)(2,1)S(1)}, bf16[256,1024]{1,0:T(8,128)(2,1)}, u32[]{:S(2)}) copy-start(bf16[256,1024]{1,0:T(8,128)(2,1)} %param.7) | copy-start | bytes 1572868
  7.2 109.1 %all-gather.5.cloned.1.call-start = ((), (), s32[]{:S(2)}) async-start(), calls=%async_computation.3 | async-start | bytes 12582912 | tf_op jit(solution)/shard_map/all_gather | solution.py:36
  7.9 213.9 %all-gather.3.cloned.1.call-start = ((), (), s32[]{:S(2)}) async-start(), calls=%async_computation.2 | async-start | bytes 12582912 | tf_op jit(solution)/shard_map/all_gather | solution.py:35
  8.7 375.5 %all-reduce.7.cloned.1.call-start = ((), (), s32[]{:S(2)}) async-start(), calls=%async_computation.6 | async-start | bytes 8388608 | tf_op jit(solution)/shard_map/psum | solution.py:38
  229.0 204.3 %all-reduce.9.cloned.1.call-start = ((), (), s32[]{:S(2)}) async-start(), calls=%async_computation.7 | async-start | bytes 2097152 | tf_op jit(solution)/shard_map/psum | solution.py:43
  384.2 3.7 copy-start.1
  384.2 10.5 %slice-start = ((s8[8388608]{0:T(1024)(128)(4,1)}), s8[4194304]{0:T(1024)(128)(4,1)S(1)}, s32[]{:S(2)}) async-start(s8[8388608]{0:T(1024)(128)(4,1)} %bitcast.8), calls=%async_computation.8 | async-start | bytes 8388608
  387.9 6.8 %slice-start.1 = ((s8[8388608]{0:T(1024)(128)(4,1)}), s8[4194304]{0:T(1024)(128)(4,1)S(1)}, s32[]{:S(2)}) async-start(s8[8388608]{0:T(1024)(128)(4,1)} %bitcast.8), calls=%async_computation.9 | async-start | bytes 8388608
  397.8 138.0 %reduce-scatter.3.cloned.1.call-start = ((), (), s32[]{:S(2)}) async-start(), calls=%async_computation.4 | async-start | bytes 12582912 | tf_op jit(solution)/shard_map/reduce_scatter | solution.py:56
  403.8 1.6 copy-start.2
  403.8 234.1 %reduce-scatter.5.cloned.1.call-start = ((), (), s32[]{:S(2)}) async-start(), calls=%async_computation.5 | async-start | bytes 12582912 | tf_op jit(solution)/shard_map/reduce_scatter | solution.py:48
Sparse Core Ops, SparseCore 0:
  9.5 106.6 all-gather.4
  117.8 103.9 all-gather.2
  229.1 155.0 all-reduce.6
  398.0 35.2 all-reduce.8
  436.0 99.7 reduce-scatter.2
  538.6 99.2 reduce-scatter.4
where the time goes:
time: 645 us
  waiting for transfers between devices  561 us (87%)
  matrix products  34.6 us (5%)
  blocking collectives  25.2 us (4%)
  between operations  14.2 us (2%)
  other arithmetic  7.98 us (1%)
    psum x1, waiting for transfers between devices, local(): lax.psum(jnp.dot(normalized_rows, up_full, preferred_element_type=jnp.flo...  155 us
    reduce_scatter x1, waiting for transfers between devices, local(): lax.psum_scatter(down_part.astype(jnp.bfloat16), 'fsdp', scatter_dimensio...  102 us
    all_gather x1, waiting for transfers between devices, local(): lax.all_gather(w_up, 'fsdp', axis=1, tiled=True)  98.5 us
    all_gather x1, waiting for transfers between devices, local(): lax.all_gather(w_down, 'fsdp', axis=0, tiled=True)  93.8 us
    reduce_scatter x1, waiting for transfers between devices, local(): lax.psum_scatter(up_part.astype(jnp.bfloat16), 'fsdp', scatter_dimension=...  86.8 us
    psum x1, waiting for transfers between devices, local(): lax.psum(jnp.dot(hidden, down_full, preferred_element_type=jnp.float32).a...  23.2 us
    dot_general x4, matrix products, contract(): lax.dot_general(left, right, (((left_dim,), (right_dim,)), ((), ())), pre...  20.7 us
    psum x1, blocking collectives, local(): lax.psum((jnp.sum(input_float, axis=1), jnp.sum(input_float * input_float...  13.5 us
  transfers between devices with their start and end apart: 6, of which 6 were waited for; matrix products, arithmetic and copies ran while one was open for 3% of the time, Pallas kernels for 0%

commit v1 on v0

--- a/solution.py
+++ b/solution.py
@@ -35,9 +35,14 @@
         lax.all_gather(w_up, "fsdp", axis=1, tiled=True),
         lax.all_gather(w_down, "fsdp", axis=0, tiled=True),
     )
-    pre_full = lax.psum(
-        jnp.dot(normalized_rows, up_full, preferred_element_type=jnp.float32).astype(jnp.bfloat16),
-        "tcol",
+    pre_full = jnp.sum(
+        lax.all_gather(
+            jnp.dot(normalized_rows, up_full, preferred_element_type=jnp.float32).astype(
+                jnp.bfloat16
+            ),
+            "tcol",
+        ),
+        axis=0,
     ).astype(jnp.float32)
     hidden = gelu_value(pre_full).astype(jnp.bfloat16)
     branch = lax.psum(

time: 645 us -> 720 us (1.12)
  waiting for transfers between devices: 561 us -> 625 us
    all_gather x0 -> x1, waiting for transfers between devices: none -> 144 us  [local(): lax.all_gather(jnp.dot(normalized_rows, up_full, preferred_element_type=j...]
    psum x1, waiting for transfers between devices: 155 us -> 75 us  [local(): lax.psum(contract(cotangent, down_full, 1, 1).astype(jnp.bfloat16), 'tcol')]
  transfers between devices with their start and end apart: 6 -> 7, of which waited for: 6 -> 7; matrix products, arithmetic and copies ran while one was open for 3% -> 6% of each run, Pallas kernels for 0% -> 0%
where the time goes in v1:
time: 720 us; the launch traced here: 719 us
  waiting for transfers between devices  625 us (87%)
  matrix products  39.9 us (6%)
  blocking collectives  25.2 us (4%)
  between operations  14.2 us (2%)
  other arithmetic  12.7 us (2%)
    all_gather x1, waiting for transfers between devices, local(): lax.all_gather(jnp.dot(normalized_rows, up_full, preferred_element_type=j...  144 us
    reduce_scatter x1, waiting for transfers between devices, local(): lax.psum_scatter(down_part.astype(jnp.bfloat16), 'fsdp', scatter_dimensio...  102 us
    all_gather x1, waiting for transfers between devices, local(): lax.all_gather(w_down, 'fsdp', axis=0, tiled=True)  98.3 us
    all_gather x1, waiting for transfers between devices, local(): lax.all_gather(w_up, 'fsdp', axis=1, tiled=True)  93.8 us
    reduce_scatter x1, waiting for transfers between devices, local(): lax.psum_scatter(up_part.astype(jnp.bfloat16), 'fsdp', scatter_dimension=...  86.8 us
    psum x1, waiting for transfers between devices, local(): lax.psum(contract(cotangent, down_full, 1, 1).astype(jnp.bfloat16), 'tcol')  75 us
    dot_general x4, matrix products, contract(): lax.dot_general(left, right, (((left_dim,), (right_dim,)), ((), ())), pre...  25.6 us
    psum x1, waiting for transfers between devices, local(): lax.psum(jnp.dot(hidden, down_full, preferred_element_type=jnp.float32).a...  23.3 us
  transfers between devices with their start and end apart: 7, of which 7 were waited for; matrix products, arithmetic and copies ran while one was open for 6% of the time, Pallas kernels for 0%

profile of v1, /device:TPU:0, one launch (start us, length us, event | category | flops | bytes accessed | tf_op | source)
XLA Modules:
  0.0 719.1 jit_solution(11233967885277707485)
XLA Ops:
  7.2 0.0 all-gather.5.cloned.1.call-start
  7.2 0.7 all-gather.5.cloned.1.call-update
  7.9 0.0 all-gather.7.cloned.1.call-start
  8.0 0.7 all-gather.7.cloned.1.call-update
  8.7 0.0 all-gather.9.cloned.1.call-start
  8.7 0.2 convert_reduce_fusion
  9.0 13.5 %all-reduce.1 = (f32[256]{0:T(256)S(1)}, f32[256]{0:T(256)S(1)}) all-reduce(f32[256]{0:T(256)S(1)} %get-tuple-element.7, f32[256]{0:T(256)S(1)} %get-tuple-element.6), channel_id=1, replica_groups=mesh['fsdp'=2,'trow'=4,'tcol'=4] {'tcol'}, use_global_device_ids=true, to_apply=%region_3.0 | all-reduce | flops 512 | bytes 4096 | tf_op jit(solution)/shard_map/psum | solution.py:26
  22.5 93.8 %all-gather.5.cloned.1.call-done = bf16[1024,4096]{1,0:T(8,128)(2,1)} async-done(((bf16[1024,2048]{1,0:T(8,128)(2,1)}), bf16[1024,4096]{1,0:T(8,128)(2,1)}) %all-gather.5.cloned.1.call-update) | async-done | bytes 8388624 | tf_op jit(solution)/shard_map/all_gather | solution.py:35
  116.3 7.2 convolution_convert_fusion.3
  123.5 0.0 all-gather.9.cloned.1.call-update
  123.5 0.0 all-reduce.6.cloned.1.call-start
  123.5 98.3 %all-gather.7.cloned.1.call-done = bf16[4096,1024]{1,0:T(8,128)(2,1)} async-done(((bf16[2048,1024]{1,0:T(8,128)(2,1)}), bf16[4096,1024]{1,0:T(8,128)(2,1)}) %all-gather.7.cloned.1.call-update) | async-done | bytes 8388624 | tf_op jit(solution)/shard_map/all_gather | solution.py:36
  221.8 7.1 convolution_convert_fusion.2
  228.9 0.0 all-reduce.6.cloned.1.call-update
  228.9 0.2 all-reduce.8.cloned.1.call-start
  229.2 144.5 %all-gather.9.cloned.1.call-done = bf16[1024,4096]{1,0:T(8,128)(2,1)} async-done(((bf16[256,4096]{1,0:T(8,128)(2,1)}), bf16[1024,4096]{1,0:T(8,128)(2,1)}) %all-gather.9.cloned.1.call-update) | async-done | bytes 8388624 | tf_op jit(solution)/shard_map/all_gather | solution.py:39
  373.6 5.2 reduce_sum.50
  378.8 7.0 convolution_convert_fusion.5
  385.8 75.0 %all-reduce.6.cloned.1.call-done = bf16[256,4096]{1,0:T(8,128)(2,1)} async-done(((bf16[256,4096]{1,0:T(8,128)(2,1)}), bf16[256,4096]{1,0:T(8,128)(2,1)}) %all-reduce.6.cloned.1.call-update) | async-done | bytes 2097168 | tf_op jit(solution)/shard_map/psum | solution.py:56
  460.8 3.3 fusion.8
  464.0 1.3 copy-done.1
  465.3 6.5 convolution_convert_fusion.4
  471.9 0.0 reduce-scatter.3.cloned.1.call-start
  472.0 7.3 %convolution_convert_fusion.1 = bf16[1024,4096]{1,0:T(8,128)(2,1)} fusion(bf16[256,4096]{1,0:T(8,128)(2,1)} %copy-done.1, bf16[256,1024]{1,0:T(8,128)(2,1)S(1)} %copy-done, f32[256]{0:T(256)S(1)} %get-tuple-element.17, f32[256]{0:T(256)S(1)} %get-tuple-element.16), kind=kOutput, calls=%fused_computation.6 | convolution fusion | flops 2152726528 | bytes 11012096 | tf_op jit(solution)/shard_map/dot_general | solution.py:18
  479.3 0.0 reduce-scatter.5.cloned.1.call-start
  479.3 4.7 convolution_convert_fusion
  484.1 23.3 %all-reduce.8.cloned.1.call-done = (bf16[256,1024]{1,0:T(8,128)(2,1)}, bf16[256,1024]{1,0:T(8,128)(2,1)}) async-done(((bf16[256,1024]{1,0:T(8,128)(2,1)}, bf16[256,1024]{1,0:T(8,128)(2,1)}), (bf16[256,1024]{1,0:T(8,128)(2,1)}, bf16[256,1024]{1,0:T(8,128)(2,1)})) %all-reduce.8.cloned.1.call-update) | async-done | bytes 1048592 | tf_op jit(solution)/shard_map/psum | solution.py:48
  507.4 1.5 convert_reduce_fusion.1
  508.9 11.7 %all-reduce = (f32[256]{0:T(256)S(1)}, f32[256]{0:T(256)S(1)}) all-reduce(f32[256]{0:T(256)S(1)} %get-tuple-element.5, f32[256]{0:T(256)S(1)} %get-tuple-element.4), channel_id=1, replica_groups=mesh['fsdp'=2,'trow'=4,'tcol'=4] {'tcol'}, use_global_device_ids=true, to_apply=%region_11.0 | all-reduce | flops 512 | bytes 4096 | tf_op jit(solution)/shard_map/psum | solution.py:67
  520.6 2.6 fusion.12
  523.2 86.8 %reduce-scatter.3.cloned.1.call-done = bf16[1024,2048]{1,0:T(8,128)(2,1)} async-done(((bf16[1024,4096]{1,0:T(8,128)(2,1)}), bf16[1024,2048]{1,0:T(8,128)(2,1)}) %reduce-scatter.3.cloned.1.call-update) | async-done | bytes 4194320 | tf_op jit(solution)/shard_map/reduce_scatter | solution.py:61
  610.0 102.2 %reduce-scatter.5.cloned.1.call-done = bf16[2048,1024]{1,0:T(8,128)(2,1)} async-done(((bf16[4096,1024]{1,0:T(8,128)(2,1)}), bf16[2048,1024]{1,0:T(8,128)(2,1)}) %reduce-scatter.5.cloned.1.call-update) | async-done | bytes 4194320 | tf_op jit(solution)/shard_map/reduce_scatter | solution.py:53
  (10 shorter events, 0.1 us)
Async XLA Ops:
  7.2 1.5 copy-start
  7.2 109.1 %all-gather.5.cloned.1.call-start = ((), (), s32[]{:S(2)}) async-start(), calls=%async_computation.2 | async-start | bytes 12582912 | tf_op jit(solution)/shard_map/all_gather | solution.py:35
  7.9 213.9 %all-gather.7.cloned.1.call-start = ((), (), s32[]{:S(2)}) async-start(), calls=%async_computation.3 | async-start | bytes 12582912 | tf_op jit(solution)/shard_map/all_gather | solution.py:36
  8.7 365.0 %all-gather.9.cloned.1.call-start = ((), (), s32[]{:S(2)}) async-start(), calls=%async_computation.7 | async-start | bytes 10485760 | tf_op jit(solution)/shard_map/all_gather | solution.py:39
  116.3 105.6 %copy-start.2 = (bf16[256,1024]{1,0:T(8,128)(2,1)S(1)}, bf16[256,1024]{1,0:T(8,128)(2,1)}, u32[]{:S(2)}) copy-start(bf16[256,1024]{1,0:T(8,128)(2,1)} %param.7) | copy-start | bytes 1572868
  123.5 337.3 %all-reduce.6.cloned.1.call-start = ((), (), s32[]{:S(2)}) async-start(), calls=%async_computation.4 | async-start | bytes 4194304 | tf_op jit(solution)/shard_map/psum | solution.py:56
  228.9 278.5 %all-reduce.8.cloned.1.call-start = ((), (), s32[]{:S(2)}) async-start(), calls=%async_computation.8 | async-start | bytes 2097152 | tf_op jit(solution)/shard_map/psum | solution.py:48
  464.0 1.3 copy-start.1
  471.9 138.1 %reduce-scatter.3.cloned.1.call-start = ((), (), s32[]{:S(2)}) async-start(), calls=%async_computation.5 | async-start | bytes 12582912 | tf_op jit(solution)/shard_map/reduce_scatter | solution.py:61
  479.3 232.9 %reduce-scatter.5.cloned.1.call-start = ((), (), s32[]{:S(2)}) async-start(), calls=%async_computation.6 | async-start | bytes 12582912 | tf_op jit(solution)/shard_map/reduce_scatter | solution.py:53
Sparse Core Ops, SparseCore 0:
  9.5 106.6 all-gather.4
  117.8 103.9 all-gather.6
  224.0 149.5 all-gather.8
  376.4 84.3 all-reduce.5
  472.0 35.3 all-reduce.7
  510.2 99.7 reduce-scatter.2
  612.9 99.3 reduce-scatter.4
